TPU v7x, 32 devices: a whole 2x2x4 slice. The times are simulated.
32 devices in a mesh: groups: 2 (over y), chan: 8 (over z, x), sub: 2 (over core).
Axes of the slice: x: 2, y: 2, z: 4, core: 2. Of those that a mesh axis runs over, the one named last changes fastest.
Arguments:
- predicted_sky_response: bfloat16 [16384, 8, 2, 128], P(('groups', 'chan', 'sub')), parts along dimension 0, may hold values from -0.4375 to 0.4375
- measured_correlation: bfloat16 [16384, 2, 128], P(('groups', 'chan', 'sub')), parts along dimension 0, may hold values from -6 to 6
- keep_indicator: int32 [16384, 128], P(('groups', 'chan', 'sub')), parts along dimension 0, may hold values 0 or 1
- tile_owner: int32 [16384, 1], P(('groups', 'chan', 'sub')), parts along dimension 0, may hold values from 0 to 7; in each aligned block of 512 rows (0 to 511, 512 to 1023, ...) at most 192 rows name the same one
- tile_channel: int32 [16384], P(('groups', 'chan', 'sub')), parts along dimension 0, may hold values from 0 to 3
- tile_base: int32 [16384], P(('groups', 'chan', 'sub')), parts along dimension 0, may hold values from 0 to 14
- pairs: int32 [15, 2, 128], replicated, may hold values from 0 to 61, as said below
- gains: float32 [64, 2, 62, 8], P(('groups', 'chan')), parts along dimension 0, may hold values from -5 to 5
- duals: float32 [64, 2, 62, 8], P(('groups', 'chan', 'sub')), parts along dimension 0, may hold values from -4 to 4
- consensus: float32 [8, 2, 62, 8], P('groups'), parts along dimension 0, may hold values from -5 to 5
- rho: float32 [8], replicated, may hold values from 0.3 to 3
Outputs:
- gains_new: float32 [64, 2, 62, 8], P(('groups', 'chan', 'sub')), parts along dimension 0
- consensus_new: float32 [8, 2, 62, 8], P('groups'), parts along dimension 0
- duals_new: float32 [64, 2, 62, 8], P(('groups', 'chan', 'sub')), parts along dimension 0
There are 2 independent parts, one for each index of `groups`. A program takes and returns all parts, laid end to end along the dimension named above; an argument that names none is the same for every part. Nothing has to cross between parts.
Inputs may be any that keep to these rules, and one draw needn't show every extreme that they name: `tile_owner`: on the tiles of one device at most 192 name the same owner, a bound that some block reaches. `pairs`: the two stations of a row differ.
All inputs are finite; a program needn't handle non-finite values. No bound on the sum of `keep_indicator` on one device may be relied on, other than what follows from the above.
Results may differ from a plain program's by a relative error of at most 0.0027.
Values may be sent and summed in bfloat16 or wider, within the bound.
A program may use at most 128 MiB of HBM per device.

v0:
```python
import math

import jax
import jax.numpy as jnp
from jax import lax
from jax.sharding import PartitionSpec as P


def legendre_rows(channels):
    positions = jnp.arange(channels, dtype=jnp.float32)
    abscissa = (2.0 * positions - (channels - 1)) / max(channels - 1, 1)
    return jnp.stack(
        [
            jnp.ones_like(abscissa),
            abscissa,
            0.5 * (3.0 * abscissa * abscissa - 1.0),
            0.5 * (5.0 * abscissa * abscissa * abscissa - 3.0 * abscissa),
        ]
    )


def outer_terms(vector_real, vector_imag, weight_real, weight_imag):
    tiles_count, row_total_count, directions = vector_real.shape
    outer_real = (
        vector_real[..., :, None] * vector_real[..., None, :]
        + vector_imag[..., :, None] * vector_imag[..., None, :]
    )
    outer_imag = (
        vector_real[..., :, None] * vector_imag[..., None, :]
        - vector_imag[..., :, None] * vector_real[..., None, :]
    )
    normal = jnp.stack([outer_real, outer_imag], axis=2).reshape(
        tiles_count, row_total_count, 2 * directions * directions
    )
    side_real = vector_real * weight_real[..., None] + vector_imag * weight_imag[..., None]
    side_imag = vector_real * weight_imag[..., None] - vector_imag * weight_real[..., None]
    right_side = jnp.stack([side_real, side_imag], axis=2).reshape(
        tiles_count, row_total_count, 2 * directions
    )
    return (normal, right_side)


def row_terms(coupling, observed, near_gain, far_gain):
    coupling_real = jnp.swapaxes(coupling[:, :, 0, :], 1, 2).astype(jnp.float32)
    coupling_imag = jnp.swapaxes(coupling[:, :, 1, :], 1, 2).astype(jnp.float32)
    near_real, near_imag = (near_gain[:, :, 0, :], near_gain[:, :, 1, :])
    far_real, far_imag = (far_gain[:, :, 0, :], far_gain[:, :, 1, :])
    slope_real = coupling_real * far_real + coupling_imag * far_imag
    slope_imag = coupling_imag * far_real - coupling_real * far_imag
    mirror_real = coupling_real * near_real - coupling_imag * near_imag
    mirror_imag = -(coupling_real * near_imag + coupling_imag * near_real)
    model_real = jnp.sum(near_real * slope_real - near_imag * slope_imag, axis=-1)
    model_imag = jnp.sum(near_real * slope_imag + near_imag * slope_real, axis=-1)
    observed_f = observed.astype(jnp.float32)
    residual_real = observed_f[:, 0, :] - model_real
    residual_imag = observed_f[:, 1, :] - model_imag
    normal_near, right_near = outer_terms(slope_real, slope_imag, residual_real, residual_imag)
    normal_far, right_far = outer_terms(mirror_real, mirror_imag, residual_real, -residual_imag)
    normal = jnp.concatenate([normal_near, normal_far], axis=1).astype(jnp.bfloat16)
    right_side = jnp.concatenate([right_near, right_far], axis=1).astype(jnp.bfloat16)
    return (normal, right_side)


def tile_normals(coupling, observed, channel_index, base_index, pairs, gain_table):
    stations_count = gain_table.shape[2]
    stations = pairs[base_index]
    station_ids = jnp.arange(stations_count, dtype=jnp.int32)
    near_onehot = (stations[:, 0, :, None] == station_ids).astype(jnp.float32)
    far_onehot = (stations[:, 1, :, None] == station_ids).astype(jnp.float32)
    tile_gains = gain_table[channel_index]
    near_gain = jnp.einsum(
        "trs,tcsk->trck", near_onehot, tile_gains, precision=lax.Precision.HIGHEST
    )
    far_gain = jnp.einsum("trs,tcsk->trck", far_onehot, tile_gains, precision=lax.Precision.HIGHEST)
    normal, right_side = row_terms(coupling, observed, near_gain, far_gain)
    both_onehot = jnp.concatenate([near_onehot, far_onehot], axis=1).astype(jnp.bfloat16)
    tile_normal = jnp.einsum(
        "trs,trc->tsc", both_onehot, normal, preferred_element_type=jnp.float32
    )
    tile_right = jnp.einsum(
        "trs,trc->tsc", both_onehot, right_side, preferred_element_type=jnp.float32
    )
    return (tile_normal, tile_right)


def accumulate(coupling, observed, channel_index, base_index, pairs, gain_table, channel_slots):
    tiles_count = coupling.shape[0]
    block_size = math.gcd(tiles_count, 32)
    iteration_tally = tiles_count // block_size
    stations_count = gain_table.shape[2]
    directions = gain_table.shape[3]

    def one_step(totals, block_item):
        normal_acc, right_acc = totals
        tile_normal, tile_right = tile_normals(
            block_item[0], block_item[1], block_item[2], block_item[3], pairs, gain_table
        )
        return (
            (
                normal_acc.at[block_item[2]].add(tile_normal),
                right_acc.at[block_item[2]].add(tile_right),
            ),
            None,
        )

    block_items = (
        coupling.reshape((iteration_tally, block_size) + coupling.shape[1:]),
        observed.reshape((iteration_tally, block_size) + observed.shape[1:]),
        channel_index.reshape(iteration_tally, block_size),
        base_index.reshape(iteration_tally, block_size),
    )
    start_totals = (
        jnp.zeros((channel_slots, stations_count, 2 * directions * directions), jnp.float32),
        jnp.zeros((channel_slots, stations_count, 2 * directions), jnp.float32),
    )
    (normal_sum, right_sum), _ = lax.scan(one_step, start_totals, block_items)
    return (normal_sum, right_sum)


def admm_update(normal, right_side, gain, dual, anchor, rho):
    count, stations = (normal.shape[0], normal.shape[1])
    directions = rho.shape[0]
    normal_blocks = normal.reshape(count, stations, 2, directions, directions)
    ridge_diag = jnp.diag(rho)
    higher_half_records = jnp.concatenate(
        [normal_blocks[:, :, 0] + ridge_diag, -normal_blocks[:, :, 1]], axis=-1
    )
    lower_rows = jnp.concatenate(
        [normal_blocks[:, :, 1], normal_blocks[:, :, 0] + ridge_diag], axis=-1
    )
    system = jnp.concatenate([higher_half_records, lower_rows], axis=-2)
    gain_rows = jnp.transpose(gain, (0, 2, 1, 3))
    dual_rows = jnp.transpose(dual, (0, 2, 1, 3))
    anchor_rows = jnp.transpose(anchor, (0, 2, 1, 3))
    target = (
        right_side.reshape(count, stations, 2, directions)
        - dual_rows
        - rho * (gain_rows - anchor_rows)
    )
    factor = jnp.linalg.cholesky(system)
    gain_step = jax.scipy.linalg.cho_solve(
        (factor, True), target.reshape(count, stations, 2 * directions)[..., None]
    )[..., 0]
    return gain + jnp.transpose(gain_step.reshape(count, stations, 2, directions), (0, 2, 1, 3))


def fit_consensus(poly_basis, summed):
    gram_matrix = jnp.dot(poly_basis, poly_basis.T, precision=lax.Precision.HIGHEST)
    factor = jnp.linalg.cholesky(gram_matrix)
    coeffs = jax.scipy.linalg.cho_solve((factor, True), summed.reshape(summed.shape[0], -1))
    return coeffs.reshape(summed.shape)


def body(
    predicted_sky_response,
    measured_correlation,
    keep_indicator,
    tile_owner,
    tile_channel,
    tile_base,
    pairs,
    gains,
    duals,
    consensus,
    rho,
):
    channels_here = gains.shape[0]
    chan_count = lax.axis_size("chan")
    sub_count = lax.axis_size("sub")
    half_count = channels_here // sub_count
    retained_selector = keep_indicator > 0
    predicted_response_kept = jnp.where(
        retained_selector[:, None, None, :],
        predicted_sky_response,
        jnp.zeros_like(predicted_sky_response),
    )
    measured_correlation_kept = jnp.where(
        retained_selector[:, None, :], measured_correlation, jnp.zeros_like(measured_correlation)
    )
    owner_index = tile_owner[:, 0]
    all_gains = lax.all_gather(gains, "chan", axis=0, tiled=True)
    full_channel = owner_index * channels_here + tile_channel
    normal_sum, right_sum = accumulate(
        predicted_response_kept,
        measured_correlation_kept,
        full_channel,
        tile_base,
        pairs,
        all_gains,
        channels_here * chan_count,
    )
    normal_part, right_part = (
        lax.psum_scatter(normal_sum, ("chan", "sub"), scatter_dimension=0, tiled=True),
        lax.psum_scatter(right_sum, ("chan", "sub"), scatter_dimension=0, tiled=True),
    )
    sub_index = lax.axis_index("sub")
    chan_index = lax.axis_index("chan")
    my_gains = lax.dynamic_slice_in_dim(gains, sub_index * half_count, half_count, 0)
    poly_basis = legendre_rows(channels_here * chan_count)
    first_channel = (chan_index * sub_count + sub_index) * half_count
    my_basis = lax.dynamic_slice_in_dim(poly_basis, first_channel, half_count, 1)
    anchor = jnp.einsum("df,dcsk->fcsk", my_basis, consensus, precision=lax.Precision.HIGHEST)
    gains_new = admm_update(normal_part, right_part, my_gains, duals, anchor, rho)
    partial_value = jnp.einsum(
        "df,fcsk->dcsk", my_basis, gains_new + duals / rho, precision=lax.Precision.HIGHEST
    )
    summed = lax.psum(partial_value, ("chan", "sub"))
    consensus_new = fit_consensus(poly_basis, summed)
    duals_new = duals + rho * (
        gains_new
        - jnp.einsum("df,dcsk->fcsk", my_basis, consensus_new, precision=lax.Precision.HIGHEST)
    )
    return (gains_new, consensus_new, duals_new)


def solution(mesh):
    placed = (
        P(("groups", "chan", "sub"), None, None, None),
        P(("groups", "chan", "sub"), None, None),
        P(("groups", "chan", "sub"), None),
        P(("groups", "chan", "sub"), None),
        P(("groups", "chan", "sub")),
        P(("groups", "chan", "sub")),
        P(),
        P(("groups", "chan"), None, None, None),
        P(("groups", "chan", "sub"), None, None, None),
        P("groups", None, None, None),
        P(),
    )
    return jax.shard_map(
        body,
        mesh=mesh,
        in_specs=placed,
        out_specs=(
            P(("groups", "chan", "sub"), None, None, None),
            P("groups", None, None, None),
            P(("groups", "chan", "sub"), None, None, None),
        ),
        check_vma=False,
    )
```

profile of v0, /device:TPU:0, one launch (start us, length us, event | category | flops | bytes accessed | tf_op | source)
XLA Modules:
  0.0 650.6 jit_solution(18375419178991925934)
XLA Ops:
  8.3 3.6 copy_select_fusion
  12.0 32.6 %all_gather.3 = f32[32,2,62,8]{2,3,1,0:T(8,128)S(1)} all-gather(f32[4,2,62,8]{2,3,1,0:T(8,128)S(1)} %copy-done.8), channel_id=1, replica_groups=mesh['groups'=2,'chan'=8,'sub'=2] {'chan'}, dimensions={0}, use_global_device_ids=true | all-gather | bytes 142848 | tf_op jit(solution)/shard_map/all_gather | solution.py:181
  44.9 224.9 %while.12 = (s32[]{:T(128)}, f32[32,62,128]{2,1,0:T(8,128)S(1)}, f32[32,62,16]{1,2,0:T(8,128)S(1)}, s32[16,32]{1,0:T(8,128)S(1)}, s32[16,32]{1,0:T(8,128)S(1)}, ...) while((s32[]{:T(128)}, f32[32,62,128]{2,1,0:T(8,128)S(1)}, ...), condition=%wide.region_5.6_spmd, body=%wide.region_0.5_spmd.sunk | while | flops 259593408 | bytes 28256220 | solution.py:116
  49.5 1.7 scatter_fusion.1
  51.7 1.3 copy.187
  54.8 2.0 fusion.100
  56.8 2.1 scatter_fusion
  63.5 1.7 scatter_fusion.1
  65.7 1.3 copy.187
  68.8 2.0 fusion.100
  70.8 2.1 scatter_fusion
  77.6 1.7 scatter_fusion.1
  79.8 1.3 copy.187
  82.9 2.0 fusion.100
  84.9 2.1 scatter_fusion
  91.6 1.7 scatter_fusion.1
  93.8 1.3 copy.187
  96.9 2.0 fusion.100
  98.9 2.1 scatter_fusion
  105.7 1.7 scatter_fusion.1
  107.9 1.3 copy.187
  111.0 2.0 fusion.100
  113.0 2.1 scatter_fusion
  119.8 1.7 scatter_fusion.1
  122.0 1.3 copy.187
  125.1 2.0 fusion.100
  127.1 2.1 scatter_fusion
  133.8 1.7 scatter_fusion.1
  136.0 1.3 copy.187
  139.1 2.0 fusion.100
  141.1 2.1 scatter_fusion
  147.9 1.7 scatter_fusion.1
  153.2 2.0 fusion.100
  155.2 2.1 scatter_fusion
  161.9 1.7 scatter_fusion.1
  167.2 2.0 fusion.100
  169.2 2.1 scatter_fusion
  176.0 1.7 scatter_fusion.1
  181.3 2.0 fusion.100
  183.3 2.1 scatter_fusion
  190.0 1.7 scatter_fusion.1
  195.3 2.0 fusion.100
  197.3 2.1 scatter_fusion
  204.1 1.7 scatter_fusion.1
  209.4 2.0 fusion.100
  211.4 2.1 scatter_fusion
  218.2 1.8 scatter_fusion.1
  223.5 2.0 fusion.100
  225.5 2.1 scatter_fusion
  232.2 1.7 scatter_fusion.1
  237.5 2.0 fusion.100
  239.5 2.1 scatter_fusion
  246.3 1.8 scatter_fusion.1
  251.6 2.0 fusion.100
  253.6 2.1 scatter_fusion
  260.4 1.7 scatter_fusion.1
  265.7 2.0 fusion.100
  267.7 2.1 scatter_fusion
  270.6 2.0 copy.113
  275.2 52.2 %reduce-scatter.5.cloned.1.call-done = f32[2,62,16]{1,2,0:T(8,128)} async-done(((f32[32,62,16]{1,2,0:T(8,128)}), f32[2,62,16]{1,2,0:T(8,128)}) %reduce-scatter.5.cloned.1.call-update) | async-done | bytes 7952 | tf_op jit(solution)/shard_map/reduce_scatter | solution.py:194
  328.5 63.5 %reduce-scatter.3.cloned.1.call-done = f32[2,62,128]{1,2,0:T(8,128)} async-done(((f32[32,62,128]{1,2,0:T(8,128)}), f32[2,62,128]{1,2,0:T(8,128)}) %reduce-scatter.3.cloned.1.call-update) | async-done | bytes 63504 | tf_op jit(solution)/shard_map/reduce_scatter | solution.py:193
  394.5 181.8 %custom-call.21 = f32[2,62,16,16]{3,2,1,0:T(8,128)S(1)} custom-call(f32[2,62,16,16]{3,2,1,0:T(8,128)S(1)} %broadcast_multiply_fusion), custom_call_target="Cholesky" | custom-call | tf_op jit(solution)/shard_map/jit(cholesky)/cholesky | solution.py:140
  577.0 5.4 custom-call.22
  583.5 57.6 %psum.7 = f32[2,62,8,4]{1,3,2,0:T(4,128)S(1)} all-reduce(f32[2,62,8,4]{1,3,2,0:T(4,128)S(1)} %copy.126), channel_id=1, replica_groups=mesh['groups'=2,'chan'=8,'sub'=2] {'chan','sub'}, use_global_device_ids=true, to_apply=%region_12.13 | all-reduce | flops 3968 | bytes 31744 | tf_op jit(solution)/shard_map/psum | solution.py:207
  (597 shorter events, 130.8 us)
Async XLA Ops:
  7.2 321.0 %copy-start = (f32[4,2,62,8]{2,3,1,0:T(8,128)S(1)}, f32[4,2,62,8]{2,3,1,0:T(8,128)}, u32[]{:S(2)}) copy-start(f32[4,2,62,8]{2,3,1,0:T(8,128)} %param.22) | copy-start | bytes 47620
  7.2 320.2 %reduce-scatter.5.cloned.1.call-start = ((), (), s32[]{:S(2)}) async-start(), calls=%async_computation.3 | async-start | bytes 278528 | tf_op jit(solution)/shard_map/reduce_scatter | solution.py:194
  8.2 3.7 copy-start.7
  8.2 3.7 copy-start.8
  8.2 36.3 %copy-start.11 = (s32[512,1]{0,1:T(1,128)S(1)}, s32[512,1]{0,1:T(1,128)}, u32[]{:S(2)}) copy-start(s32[512,1]{0,1:T(1,128)} %param.16) | copy-start | bytes 6148
  8.3 36.3 %copy-start.9 = (s32[512]{0:T(512)S(1)}, s32[512]{0:T(512)}, u32[]{:S(2)}) copy-start(s32[512]{0:T(512)} %param.17) | copy-start | bytes 6148
  8.3 36.4 %copy-start.10 = (s32[512]{0:T(512)S(1)}, s32[512]{0:T(512)}, u32[]{:S(2)}) copy-start(s32[512]{0:T(512)} %param.18) | copy-start | bytes 6148
  11.9 33.0 %copy-start.4 = (s32[15,2,128]{2,1,0:T(2,128)S(1)}, s32[15,2,128]{2,1,0:T(2,128)}, u32[]{:S(2)}) copy-start(s32[15,2,128]{2,1,0:T(2,128)} %param.19) | copy-start | bytes 46084
  44.9 3.7 copy-start.5
  49.1 2.1 copy-start.2
  56.7 2.2 copy-start.6
  58.9 3.7 copy-start.5
  63.2 2.1 copy-start.2
  67.4 1.5 copy-start.3
  70.8 2.2 copy-start.6
  73.0 3.7 copy-start.5
  77.2 2.1 copy-start.2
  84.9 2.2 copy-start.6
  87.0 3.7 copy-start.5
  91.3 2.1 copy-start.2
  95.5 1.5 copy-start.3
  98.9 2.2 copy-start.6
  101.1 3.7 copy-start.5
  105.3 2.1 copy-start.2
  113.0 2.2 copy-start.6
  115.2 3.7 copy-start.5
  119.4 2.1 copy-start.2
  123.6 1.5 copy-start.3
  127.0 2.2 copy-start.6
  129.2 3.7 copy-start.5
  133.4 2.1 copy-start.2
  137.7 1.5 copy-start.3
  141.1 2.2 copy-start.6
  143.3 3.7 copy-start.5
  147.5 2.1 copy-start.2
  155.2 2.2 copy-start.6
  157.3 3.7 copy-start.5
  161.6 2.1 copy-start.2
  165.8 1.5 copy-start.3
  169.2 2.2 copy-start.6
  171.4 3.7 copy-start.5
  175.6 2.1 copy-start.2
  183.3 2.2 copy-start.6
  185.4 3.7 copy-start.5
  189.7 2.1 copy-start.2
  197.3 2.2 copy-start.6
  199.5 3.7 copy-start.5
  203.7 2.1 copy-start.2
  211.4 2.2 copy-start.6
  213.6 3.7 copy-start.5
  217.8 2.1 copy-start.2
  225.4 2.2 copy-start.6
  227.6 3.7 copy-start.5
  231.9 2.1 copy-start.2
  239.5 2.2 copy-start.6
  241.7 3.7 copy-start.5
  245.9 2.1 copy-start.2
  253.6 2.2 copy-start.6
  255.8 3.7 copy-start.5
  260.0 2.1 copy-start.2
  267.6 2.2 copy-start.6
  270.6 121.5 %reduce-scatter.3.cloned.1.call-start = ((), (), s32[]{:S(2)}) async-start(), calls=%async_computation.2 | async-start | bytes 2228224 | tf_op jit(solution)/shard_map/reduce_scatter | solution.py:193
  270.6 4.5 copy-start.12
  270.6 57.5 %copy-start.13 = (f32[2,2,62,8]{2,3,1,0:T(8,128)S(1)}, f32[2,2,62,8]{2,3,1,0:T(8,128)}, u32[]{:S(2)}) copy-start(f32[2,2,62,8]{2,3,1,0:T(8,128)} %param.21) | copy-start | bytes 23812
  (12 other events, 16.7 us)
Sparse Core Ops, SparseCore 0:
  270.7 56.6 reduce-scatter.4
  331.1 60.8 reduce-scatter.2
where the time goes:
time: 652 us; the launch traced here: 651 us
  other arithmetic  281 us (43%)
  waiting for transfers between devices  116 us (18%)
  blocking collectives  90.2 us (14%)
  local copies, waits for them, and re-layouts  85.5 us (13%)
  matrix products  59.6 us (9%)
  between operations  14.4 us (2%)
    another operation x4, other arithmetic, admm_update(): factor = jnp.linalg.cholesky(system)  182 us
    reduce_scatter x1, waiting for transfers between devices, body(): lax.psum_scatter(normal_sum, ('chan', 'sub'), scatter_dimension=0, tiled=...  63.5 us
    psum x1, blocking collectives, body(): summed = lax.psum(partial_value, ('chan', 'sub'))  57.6 us
    reduce_scatter x1, waiting for transfers between devices, body(): lax.psum_scatter(right_sum, ('chan', 'sub'), scatter_dimension=0, tiled=T...  52.2 us
    reshape x32, local copies, waits for them, and re-layouts, outer_terms(): jnp.stack([outer_real, outer_imag], axis=2)  42.6 us
    scatter-add x16, other arithmetic, one_step(): normal_acc.at[block_item[2]].add(tile_normal)  34.1 us
    all_gather x1, blocking collectives, body(): all_gains = lax.all_gather(gains, 'chan', axis=0, tiled=True)  32.6 us
    dot_general x16, matrix products, tile_normals(): jnp.einsum('trs,trc->tsc', both_onehot, normal, preferred_element_type=jn...  31.6 us
  transfers between devices with their start and end apart: 2, of which 2 were waited for; matrix products, arithmetic and copies ran while one was open for 1% of the time, Pallas kernels for 0%

commit v1 on v0

v1 whole, which is shorter than its diff:
```python
import functools

import jax
import jax.numpy as jnp
from jax import lax
from jax.experimental import pallas as pl
from jax.experimental.pallas import tpu as pltpu
from jax.sharding import PartitionSpec as P

LANES = 128


def legendre_rows(channels):
    positions = jnp.arange(channels, dtype=jnp.float32)
    abscissa = (2.0 * positions - (channels - 1)) / max(channels - 1, 1)
    return jnp.stack(
        [
            jnp.ones_like(abscissa),
            abscissa,
            0.5 * (3.0 * abscissa * abscissa - 1.0),
            0.5 * (5.0 * abscissa * abscissa * abscissa - 3.0 * abscissa),
        ]
    )


def hermitian_rows(real, imag, upper):
    half = real.shape[0] // 2
    groups_real = [real * real + imag * imag]
    groups_imag = []
    for shift in range(1, half + 1):
        turned_real = pltpu.roll(real, 2 * half - shift, axis=0)
        turned_imag = pltpu.roll(imag, 2 * half - shift, axis=0)
        groups_real.append(real * turned_real + imag * turned_imag)
        groups_imag.append(real * turned_imag - imag * turned_real)
    mixed = jnp.where(upper, groups_real.pop(), groups_imag.pop())
    return groups_real + groups_imag + [mixed]


def accumulate_kernel(
    block,
    unroll,
    half,
    stations,
    channel_ref,
    base_ref,
    coupling_ref,
    observed_ref,
    keep_ref,
    pairs_ref,
    gains_ref,
    out_ref,
    table,
    turned,
    coupling_f,
    observed_f,
    keep_f,
):
    step = pl.program_id(0)
    bases = pairs_ref.shape[0] // 2
    tile_rows = keep_ref.shape[1]
    width = LANES // half
    directions = gains_ref.shape[1]

    @pl.when(step == 0)
    def _():
        out_ref[...] = jnp.zeros_like(out_ref)
        turned[...] = jnp.zeros_like(turned)
        turned[: 2 * bases, :] = pairs_ref[...].astype(jnp.float32)
        columns = jnp.transpose(turned[...])
        lane = lax.broadcasted_iota(jnp.int32, (tile_rows, LANES), 1).astype(jnp.float32)
        for base in range(bases):
            for end in range(2):
                station = columns[:, 2 * base + end : 2 * base + end + 1]
                for part in range(half):
                    table[base * half + part, end * tile_rows : (end + 1) * tile_rows, :] = (
                        jnp.where(station + float(part * width) == lane, 1.0, 0.0).astype(jnp.bfloat16)
                    )

    coupling_f[...] = coupling_ref[...].astype(jnp.float32)
    observed_f[...] = observed_ref[...].astype(jnp.float32)
    keep_f[...] = jnp.where(keep_ref[...] > 0, 1.0, 0.0)
    upper = lax.broadcasted_iota(jnp.int32, (directions, LANES), 0) < directions // 2

    def spread(row):
        return jnp.broadcast_to(row, (directions, LANES))

    def one_tile(local):
        tile = step * block + local
        channel = channel_ref[tile]
        base = base_ref[tile]
        kept = spread(keep_f[pl.ds(local, 1), :])
        first = local * 2 * directions
        real = coupling_f[pl.ds(first, directions, stride=2), :] * kept
        imag = coupling_f[pl.ds(first + 1, directions, stride=2), :] * kept
        seen_real = spread(observed_f[pl.ds(2 * local, 1), :])
        seen_imag = spread(observed_f[pl.ds(2 * local + 1, 1), :])
        near = spread(pairs_ref[pl.ds(2 * base, 1), :])
        far = spread(pairs_ref[pl.ds(2 * base + 1, 1), :])
        gain_real = gains_ref[2 * channel]
        gain_imag = gains_ref[2 * channel + 1]

        def pick(values, index):
            return jnp.take_along_axis(values, index, axis=1, mode="promise_in_bounds")

        near_real, near_imag = pick(gain_real, near), pick(gain_imag, near)
        far_real, far_imag = pick(gain_real, far), pick(gain_imag, far)
        slope_real = real * far_real + imag * far_imag
        slope_imag = imag * far_real - real * far_imag
        mirror_real = real * near_real - imag * near_imag
        mirror_imag = -(real * near_imag + imag * near_real)

        def end_rows(vector_real, vector_imag, weight_real, weight_imag):
            side_real = vector_real * weight_real + vector_imag * weight_imag
            side_imag = vector_real * weight_imag - vector_imag * weight_real
            groups = hermitian_rows(vector_real, vector_imag, upper)
            whole = jnp.concatenate(groups, axis=0).astype(jnp.bfloat16)
            side = jnp.concatenate([side_real, side_imag], axis=0)
            high = side.astype(jnp.bfloat16)
            low = (side - high.astype(jnp.float32)).astype(jnp.bfloat16)
            return jnp.concatenate([whole, high, low], axis=0)

        rows = jnp.concatenate(
            [
                end_rows(slope_real, slope_imag, seen_real, seen_imag),
                end_rows(mirror_real, mirror_imag, seen_real, -seen_imag),
            ],
            axis=1,
        )
        place = lax.rem(channel, half)
        sums = jnp.dot(rows, table[base * half + place], preferred_element_type=jnp.float32)
        normal_rows = directions * directions
        return lax.div(channel, half), jnp.concatenate(
            [
                sums[:normal_rows],
                sums[normal_rows : normal_rows + 2 * directions] + sums[normal_rows + 2 * directions :],
            ],
            axis=0,
        )

    def one_group(group, carry):
        results = [one_tile(group * unroll + number) for number in range(unroll)]
        for owner, sums in results:
            out_ref[owner] += sums
        return carry

    lax.fori_loop(0, block // unroll, one_group, 0)


def accumulate(coupling, observed, keep, channel, base, pairs, gain_table, half, stations):
    tiles, directions, _, tile_rows = coupling.shape
    channels = gain_table.shape[0] // 2
    bases = pairs.shape[0]
    block = min(64, tiles)
    unroll = 8
    kernel = functools.partial(accumulate_kernel, block, unroll, half, stations)
    out_rows = directions * directions + 2 * directions
    return pl.pallas_call(
        kernel,
        grid_spec=pltpu.PrefetchScalarGridSpec(
            num_scalar_prefetch=2,
            grid=(tiles // block,),
            in_specs=[
                pl.BlockSpec((block * 2 * directions, tile_rows), lambda i, *_: (i, 0)),
                pl.BlockSpec((block * 2, tile_rows), lambda i, *_: (i, 0)),
                pl.BlockSpec((block, tile_rows), lambda i, *_: (i, 0)),
                pl.BlockSpec((2 * bases, tile_rows), lambda i, *_: (0, 0)),
                pl.BlockSpec(gain_table.shape, lambda i, *_: (0, 0, 0)),
            ],
            out_specs=pl.BlockSpec(
                (channels // half, out_rows, LANES), lambda i, *_: (0, 0, 0)
            ),
            scratch_shapes=[
                pltpu.VMEM((bases * half, 2 * tile_rows, LANES), jnp.bfloat16),
                pltpu.VMEM((LANES, tile_rows), jnp.float32),
                pltpu.VMEM((block * 2 * directions, tile_rows), jnp.float32),
                pltpu.VMEM((block * 2, tile_rows), jnp.float32),
                pltpu.VMEM((block, tile_rows), jnp.float32),
            ],
        ),
        out_shape=jax.ShapeDtypeStruct((channels // half, out_rows, LANES), jnp.float32),
        compiler_params=pltpu.CompilerParams(
            dimension_semantics=("arbitrary",), vmem_limit_bytes=60 << 20
        ),
    )(
        channel,
        base,
        coupling.reshape(tiles * 2 * directions, tile_rows),
        observed.reshape(tiles * 2, tile_rows),
        keep,
        pairs.reshape(2 * bases, tile_rows),
        gain_table,
    )


def unpack_normal(packed, directions):
    half = directions // 2
    groups = packed[: directions * directions].reshape(directions, directions, -1)
    mixed = groups[-1]
    real = [groups[d] for d in range(half)]
    imag = [jnp.zeros_like(groups[0])] + [groups[half + d] for d in range(half - 1)]
    real.append(jnp.concatenate([mixed[:half], mixed[:half]], axis=0))
    imag.append(jnp.concatenate([-mixed[half:], mixed[half:]], axis=0))
    out_real, out_imag = [], []
    for k in range(directions):
        row_real, row_imag = [], []
        for l in range(directions):
            d = (l - k) % directions
            if d <= half:
                row_real.append(real[d][k])
                row_imag.append(imag[d][k])
            else:
                row_real.append(real[directions - d][l])
                row_imag.append(-imag[directions - d][l])
        out_real.append(jnp.stack(row_real))
        out_imag.append(jnp.stack(row_imag))
    return jnp.stack(out_real), jnp.stack(out_imag)


def fit_consensus(poly_basis, summed):
    gram_matrix = jnp.dot(poly_basis, poly_basis.T, precision=lax.Precision.HIGHEST)
    factor = jnp.linalg.cholesky(gram_matrix)
    coeffs = jax.scipy.linalg.cho_solve((factor, True), summed.reshape(summed.shape[0], -1))
    return coeffs.reshape(summed.shape)


def body(
    predicted_sky_response,
    measured_correlation,
    keep_indicator,
    tile_owner,
    tile_channel,
    tile_base,
    pairs,
    gains,
    duals,
    consensus,
    rho,
):
    channels_here, _, stations, directions = gains.shape
    chan_count = lax.axis_size("chan")
    sub_count = lax.axis_size("sub")
    half = channels_here // sub_count
    turned = jnp.swapaxes(gains, 2, 3)
    turned = jnp.pad(turned, ((0, 0), (0, 0), (0, 0), (0, LANES - stations)))
    all_gains = lax.all_gather(turned, "chan", axis=0, tiled=True)
    full_channel = tile_owner[:, 0] * channels_here + tile_channel
    packed = accumulate(
        predicted_sky_response,
        measured_correlation,
        keep_indicator,
        full_channel,
        tile_base,
        pairs,
        all_gains.reshape(-1, directions, LANES),
        half,
        stations,
    )
    mine = lax.psum_scatter(packed, ("chan", "sub"), scatter_dimension=0, tiled=True)[0]
    sub_index = lax.axis_index("sub")
    chan_index = lax.axis_index("chan")
    poly_basis = legendre_rows(channels_here * chan_count)
    first_channel = (chan_index * sub_count + sub_index) * half
    my_basis = lax.dynamic_slice_in_dim(poly_basis, first_channel, half, 1)
    anchor = jnp.einsum("df,dcsk->fcsk", my_basis, consensus, precision=lax.Precision.HIGHEST)
    real, imag = unpack_normal(mine, directions)
    width = LANES // half

    def by_station(x):
        x = x.reshape(x.shape[:-1] + (half, width))[..., :stations]
        return jnp.moveaxis(x, (-2, -1), (0, 1))

    real, imag = by_station(real), by_station(imag)
    ridge = jnp.diag(rho)
    system = jnp.concatenate(
        [
            jnp.concatenate([real + ridge, -imag], axis=-1),
            jnp.concatenate([imag, real + ridge], axis=-1),
        ],
        axis=-2,
    )
    side = by_station(mine[directions * directions :].reshape(2, directions, LANES))
    duals_rows = jnp.transpose(duals, (0, 2, 1, 3))
    anchor_rows = jnp.transpose(anchor, (0, 2, 1, 3))
    target = side - duals_rows + rho * anchor_rows
    factor = jnp.linalg.cholesky(system)
    solved = jax.scipy.linalg.cho_solve(
        (factor, True), target.reshape(half, stations, 2 * directions)[..., None]
    )[..., 0]
    gains_new = jnp.transpose(solved.reshape(half, stations, 2, directions), (0, 2, 1, 3))
    partial_value = jnp.einsum(
        "df,fcsk->dcsk", my_basis, gains_new + duals / rho, precision=lax.Precision.HIGHEST
    )
    summed = lax.psum(partial_value, ("chan", "sub"))
    consensus_new = fit_consensus(poly_basis, summed)
    duals_new = duals + rho * (
        gains_new
        - jnp.einsum("df,dcsk->fcsk", my_basis, consensus_new, precision=lax.Precision.HIGHEST)
    )
    return (gains_new, consensus_new, duals_new)


def solution(mesh):
    placed = (
        P(("groups", "chan", "sub"), None, None, None),
        P(("groups", "chan", "sub"), None, None),
        P(("groups", "chan", "sub"), None),
        P(("groups", "chan", "sub"), None),
        P(("groups", "chan", "sub")),
        P(("groups", "chan", "sub")),
        P(),
        P(("groups", "chan"), None, None, None),
        P(("groups", "chan", "sub"), None, None, None),
        P("groups", None, None, None),
        P(),
    )
    return jax.shard_map(
        body,
        mesh=mesh,
        in_specs=placed,
        out_specs=(
            P(("groups", "chan", "sub"), None, None, None),
            P("groups", None, None, None),
            P(("groups", "chan", "sub"), None, None, None),
        ),
        check_vma=False,
    )
```

time: 652 us -> 400 us (0.61)
  other arithmetic: 281 us -> 193 us
  local copies, waits for them, and re-layouts: 85.5 us -> 16 us
  waiting for transfers between devices: 116 us -> 55.1 us
  matrix products: 59.6 us -> 1.49 us
  Pallas kernels: 0 us -> 26.9 us
    scatter-add x32 -> x0, other arithmetic: 62 us -> none  [the longest x16 34.1 us: one_step(): normal_acc.at[block_item[2]].add(tile_normal)]
    reduce_scatter x2 -> x1, waiting for transfers between devices: 116 us -> 55.1 us  [body(): lax.psum_scatter(packed, ('chan', 'sub'), scatter_dimension=0, tiled=True)]
    reshape x34 -> x1, local copies, waits for them, and re-layouts: 42.8 us -> 1.33 us  [accumulate(): pairs.reshape(2 * bases, tile_rows)]
    dot_general x32 -> x0, matrix products: 37.5 us -> none  [the longest x16 31.6 us: tile_normals(): jnp.einsum('trs,trc->tsc', both_onehot, normal, preferred_element_type=jn...]
    pallas_call x0 -> x1, Pallas kernels: none -> 26.9 us  [accumulate(): pl.pallas_call(kernel, grid_spec=pltpu.PrefetchScalarGridSpec(num_scalar_...]
    while x32 -> x0, matrix products: 20.6 us -> none
    gather x32 -> x0, local copies, waits for them, and re-layouts: 19.1 us -> none  [the longest x16 9.74 us: tile_normals(): stations = pairs[base_index]]
    another operation x103 -> x7, other arithmetic: 203 us -> 187 us  [the longest x4 182 us: body(): factor = jnp.linalg.cholesky(system)]
  transfers between devices with their start and end apart: 2 -> 1, of which waited for: 2 -> 1; matrix products, arithmetic and copies ran while one was open for 1% -> 1% of each run, Pallas kernels for 0% -> 0%
where the time goes in v1:
time: 400 us; the launch traced here: 399 us
  other arithmetic  193 us (48%)
  blocking collectives  92.2 us (23%)
  waiting for transfers between devices  55.1 us (14%)
  Pallas kernels  26.9 us (7%)
  local copies, waits for them, and re-layouts  16 us (4%)
  between operations  14.5 us (4%)
    another operation x4, other arithmetic, body(): factor = jnp.linalg.cholesky(system)  182 us
    psum x1, blocking collectives, body(): summed = lax.psum(partial_value, ('chan', 'sub'))  57.6 us
    reduce_scatter x1, waiting for transfers between devices, body(): lax.psum_scatter(packed, ('chan', 'sub'), scatter_dimension=0, tiled=True)  55.1 us
    all_gather x1, blocking collectives, body(): all_gains = lax.all_gather(turned, 'chan', axis=0, tiled=True)  34.5 us
    pallas_call x1, Pallas kernels, accumulate(): pl.pallas_call(kernel, grid_spec=pltpu.PrefetchScalarGridSpec(num_scalar_...  26.9 us
  transfers between devices with their start and end apart: 1, of which 1 were waited for; matrix products, arithmetic and copies ran while one was open for 1% of the time, Pallas kernels for 0%

profile of v1, /device:TPU:0, one launch (start us, length us, event | category | flops | bytes accessed | tf_op | source)
XLA Modules:
  0.0 399.1 jit_solution(11343083046875406244)
XLA Ops:
  7.2 0.7 broadcast_multiply_fusion.1
  7.9 1.3 reshape.764.pairs_ref
  9.2 0.8 pad.4
  10.0 34.5 %all_gather.3 = f32[32,2,8,128]{3,2,1,0:T(8,128)} all-gather(f32[4,2,8,128]{3,2,1,0:T(8,128)S(1)} %pad.4), channel_id=1, replica_groups=mesh['groups'=2,'chan'=8,'sub'=2] {'chan'}, dimensions={0}, use_global_device_ids=true | all-gather | bytes 294912 | tf_op jit(solution)/shard_map/all_gather | solution.py:245
  44.6 1.3 add.93.channel_ref
  45.8 26.9 %shard_map.130 = f32[16,80,128]{2,1,0:T(8,128)} custom-call(s32[512]{0:T(512)} %add.93.channel_ref, s32[512]{0:T(512)} %base_ref.1, bf16[8192,128]{1,0:T(8,128)(2,1)} %bitcast.200, bf16[1024,128]{1,0:T(8,128)(2,1)} %bitcast.202, s32[512,128]{1,0:T(8,128)} %keep_ref.1, s32[30,128]{1,0:T(8,128)} %reshape.764.pairs_ref, f32[64,8,128]{2,1,0:T(8,128)} %bitcast.201), custom_call_target="tpu_custom_call" | custom-call | tf_op jit(solution)/shard_map/pallas_call | solution.py:157
  72.9 0.1 fusion.31
  73.0 0.1 copy.553
  73.1 0.4 cholesky.62
  73.5 0.6 compare_reduce_fusion.1
  74.1 0.6 fusion.13
  74.8 0.3 custom-call.23
  75.2 55.1 %reduce-scatter.2.cloned.1.call-done = f32[1,80,128]{2,1,0:T(8,128)} async-done(((f32[16,80,128]{2,1,0:T(8,128)}), f32[1,80,128]{2,1,0:T(8,128)}) %reduce-scatter.2.cloned.1.call-update) | async-done | bytes 40976 | tf_op jit(solution)/shard_map/reduce_scatter | solution.py:258
  130.4 0.7 slice_negate_fusion
  131.0 0.8 slice_reduce_fusion.54
  131.8 0.1 stack.275
  132.2 0.9 slice_reduce_fusion
  133.1 0.1 stack.304
  133.4 0.1 stack.295
  133.5 0.1 stack.294
  133.6 0.1 stack.293
  133.7 0.1 stack.289
  133.7 0.1 stack.288
  133.8 0.1 stack.287
  133.9 0.1 squeeze.17
  134.0 0.1 stack.284
  134.1 0.1 stack.283
  134.2 0.1 stack.282
  134.2 0.1 squeeze.16
  134.4 0.1 stack.301
  134.5 0.1 stack.297
  134.7 0.9 slice_reduce_fusion.18
  135.6 0.1 squeeze.15
  135.7 0.1 stack.279
  135.7 0.1 stack.278
  135.8 0.1 stack.277
  135.9 0.1 squeeze.14
  136.0 0.1 squeeze.13
  136.1 0.1 squeeze.12
  136.8 0.1 stack.236
  137.7 0.7 slice.613
  138.4 0.1 reshape_reshape.3
  138.5 0.3 fusion.3
  138.8 0.9 slice_reduce_fusion.36
  139.7 0.1 stack.257
  142.3 0.2 bitcast_add_fusion
  142.4 0.5 copy.547
  143.0 181.8 %custom-call.21 = f32[2,62,16,16]{3,2,1,0:T(8,128)S(1)} custom-call(f32[2,62,16,16]{3,2,1,0:T(8,128)S(1)} %broadcast_multiply_fusion), custom_call_target="Cholesky" | custom-call | tf_op jit(solution)/shard_map/jit(cholesky)/cholesky | solution.py:285
  324.8 0.5 copy.548
  325.3 0.1 select_reduce_fusion
  325.4 0.1 select_bitcast_fusion
  325.5 5.4 %custom-call.22 = f32[2,62,1,16,16]{1,3,4,2,0:T(8,128)S(1)} custom-call(f32[2,62,1,16,16]{1,4,3,2,0:T(8,128)S(1)} %select_bitcast_fusion), custom_call_target="InvertDiagBlocksLowerTriangular" | custom-call | tf_op jit(solution)/shard_map/jit(_cho_solve)/vmap(vmap())/triangular_solve | solution.py:286
  331.1 0.6 copy.560
  331.7 0.3 fusion.9
  332.0 0.2 copy.556
  332.1 0.2 reshape.767
  332.3 0.1 triangular_solve.86
  332.5 0.1 copy.557
  332.6 57.6 %psum.7 = f32[2,62,8,4]{1,3,2,0:T(4,128)S(1)} all-reduce(f32[2,62,8,4]{1,3,2,0:T(4,128)S(1)} %copy.557), channel_id=1, replica_groups=mesh['groups'=2,'chan'=8,'sub'=2] {'chan','sub'}, use_global_device_ids=true, to_apply=%region_5.6 | all-reduce | flops 3968 | bytes 31744 | tf_op jit(solution)/shard_map/psum | solution.py:293
  390.2 0.2 fusion.17
  390.5 0.2 fusion.19
  390.7 0.3 fusion.1
  391.0 0.6 copy.561
  391.6 0.6 copy.562
  (128 shorter events, 4.8 us)
Async XLA Ops:
  7.2 131.3 %copy-start = (f32[4,2,62,8]{2,3,1,0:T(8,128)S(1)}, f32[4,2,62,8]{2,3,1,0:T(8,128)}, u32[]{:S(2)}) copy-start(f32[4,2,62,8]{2,3,1,0:T(8,128)} %param.20) | copy-start | bytes 47620
  7.2 123.2 %reduce-scatter.2.cloned.1.call-start = ((), (), s32[]{:S(2)}) async-start(), calls=%async_computation.1 | async-start | bytes 696320 | tf_op jit(solution)/shard_map/reduce_scatter | solution.py:258
  45.8 29.3 %copy-start.1 = (f32[8]{0:T(128)S(1)}, f32[8]{0:T(128)}, u32[]{:S(2)}) copy-start(f32[8]{0:T(128)} %param.21) | copy-start | bytes 100
  45.8 92.6 %copy-start.2 = (f32[2,2,62,8]{2,3,1,0:T(8,128)S(1)}, f32[2,2,62,8]{2,3,1,0:T(8,128)}, u32[]{:S(2)}) copy-start(f32[2,2,62,8]{2,3,1,0:T(8,128)} %param.19) | copy-start | bytes 23812
Sparse Core Ops, SparseCore 0:
  72.9 57.4 reduce-scatter.1

commit v2 on v1

--- a/solution.py
+++ b/solution.py
@@ -2,25 +2,13 @@
 
 import jax
 import jax.numpy as jnp
+import numpy as np
 from jax import lax
 from jax.experimental import pallas as pl
 from jax.experimental.pallas import tpu as pltpu
 from jax.sharding import PartitionSpec as P
 
 LANES = 128
-
-
-def legendre_rows(channels):
-    positions = jnp.arange(channels, dtype=jnp.float32)
-    abscissa = (2.0 * positions - (channels - 1)) / max(channels - 1, 1)
-    return jnp.stack(
-        [
-            jnp.ones_like(abscissa),
-            abscissa,
-            0.5 * (3.0 * abscissa * abscissa - 1.0),
-            0.5 * (5.0 * abscissa * abscissa * abscissa - 3.0 * abscissa),
-        ]
-    )
 
 
 def hermitian_rows(real, imag, upper):
@@ -40,7 +28,6 @@
     block,
     unroll,
     half,
-    stations,
     channel_ref,
     base_ref,
     coupling_ref,
@@ -96,8 +83,11 @@
         seen_imag = spread(observed_f[pl.ds(2 * local + 1, 1), :])
         near = spread(pairs_ref[pl.ds(2 * base, 1), :])
         far = spread(pairs_ref[pl.ds(2 * base + 1, 1), :])
-        gain_real = gains_ref[2 * channel]
-        gain_imag = gains_ref[2 * channel + 1]
+        place = lax.rem(channel, half)
+        owner = lax.div(channel, half)
+        near, far = near + place * width, far + place * width
+        gain_real = gains_ref[2 * owner]
+        gain_imag = gains_ref[2 * owner + 1]
 
         def pick(values, index):
             return jnp.take_along_axis(values, index, axis=1, mode="promise_in_bounds")
@@ -126,10 +116,9 @@
             ],
             axis=1,
         )
-        place = lax.rem(channel, half)
         sums = jnp.dot(rows, table[base * half + place], preferred_element_type=jnp.float32)
         normal_rows = directions * directions
-        return lax.div(channel, half), jnp.concatenate(
+        return owner, jnp.concatenate(
             [
                 sums[:normal_rows],
                 sums[normal_rows : normal_rows + 2 * directions] + sums[normal_rows + 2 * directions :],
@@ -146,13 +135,13 @@
     lax.fori_loop(0, block // unroll, one_group, 0)
 
 
-def accumulate(coupling, observed, keep, channel, base, pairs, gain_table, half, stations):
+def accumulate(coupling, observed, keep, channel, base, pairs, gain_table, half):
     tiles, directions, _, tile_rows = coupling.shape
-    channels = gain_table.shape[0] // 2
+    owners = gain_table.shape[0] // 2
     bases = pairs.shape[0]
     block = min(64, tiles)
     unroll = 8
-    kernel = functools.partial(accumulate_kernel, block, unroll, half, stations)
+    kernel = functools.partial(accumulate_kernel, block, unroll, half)
     out_rows = directions * directions + 2 * directions
     return pl.pallas_call(
         kernel,
@@ -167,7 +156,7 @@
                 pl.BlockSpec(gain_table.shape, lambda i, *_: (0, 0, 0)),
             ],
             out_specs=pl.BlockSpec(
-                (channels // half, out_rows, LANES), lambda i, *_: (0, 0, 0)
+                (owners, out_rows, LANES), lambda i, *_: (0, 0, 0)
             ),
             scratch_shapes=[
                 pltpu.VMEM((bases * half, 2 * tile_rows, LANES), jnp.bfloat16),
@@ -177,7 +166,7 @@
                 pltpu.VMEM((block, tile_rows), jnp.float32),
             ],
         ),
-        out_shape=jax.ShapeDtypeStruct((channels // half, out_rows, LANES), jnp.float32),
+        out_shape=jax.ShapeDtypeStruct((owners, out_rows, LANES), jnp.float32),
         compiler_params=pltpu.CompilerParams(
             dimension_semantics=("arbitrary",), vmem_limit_bytes=60 << 20
         ),
@@ -192,35 +181,331 @@
     )
 
 
-def unpack_normal(packed, directions):
-    half = directions // 2
-    groups = packed[: directions * directions].reshape(directions, directions, -1)
-    mixed = groups[-1]
-    real = [groups[d] for d in range(half)]
-    imag = [jnp.zeros_like(groups[0])] + [groups[half + d] for d in range(half - 1)]
-    real.append(jnp.concatenate([mixed[:half], mixed[:half]], axis=0))
-    imag.append(jnp.concatenate([-mixed[half:], mixed[half:]], axis=0))
-    out_real, out_imag = [], []
+def lay_pair(load, pad, half, width):
+    total = None
+    for part in range(half):
+        block = load(part)
+        pad[part % 2, :, : block.shape[1]] = block
+        value = pad[part % 2]
+        if part:
+            value = pltpu.roll(value, part * width, axis=1)
+        total = value if total is None else total + value
+    return total
+
+
+def gather_kernel(chan_count, sub_count, half, gains_ref, out_ref, pad, send_sem, recv_sem):
+    chan = lax.axis_index("chan")
+    width = LANES // half
+    pad[...] = jnp.zeros_like(pad)
+    for owner in range(sub_count):
+        for part in range(2):
+            out_ref[chan, owner, part] = lay_pair(
+                lambda number: gains_ref[owner * half + number, part], pad, half, width
+            )
+    barrier = pltpu.get_barrier_semaphore()
+    for offset in range(1, chan_count):
+        pl.semaphore_signal(
+            barrier,
+            inc=1,
+            device_id={"chan": lax.rem(chan + offset, chan_count)},
+            device_id_type=pl.DeviceIdType.MESH,
+        )
+    pl.semaphore_wait(barrier, chan_count - 1)
+    copies = []
+    for offset in range(1, chan_count):
+        copy = pltpu.make_async_remote_copy(
+            src_ref=out_ref.at[chan],
+            dst_ref=out_ref.at[chan],
+            send_sem=send_sem.at[offset],
+            recv_sem=recv_sem.at[offset],
+            device_id={"chan": lax.rem(chan + offset, chan_count)},
+            device_id_type=pl.DeviceIdType.MESH,
+        )
+        copy.start()
+        copies.append(copy)
+    for copy in copies:
+        copy.wait()
+
+
+def gather_gains(gains, chan_count, sub_count):
+    channels_here, _, directions, _ = gains.shape
+    half = channels_here // sub_count
+    return pl.pallas_call(
+        functools.partial(gather_kernel, chan_count, sub_count, half),
+        out_shape=jax.ShapeDtypeStruct(
+            (chan_count, sub_count, 2, directions, LANES), jnp.float32
+        ),
+        in_specs=[pl.BlockSpec(memory_space=pltpu.VMEM)],
+        out_specs=pl.BlockSpec(memory_space=pltpu.VMEM),
+        scratch_shapes=[
+            pltpu.VMEM((2, directions, LANES), jnp.float32),
+            pltpu.SemaphoreType.DMA((chan_count,)),
+            pltpu.SemaphoreType.DMA((chan_count,)),
+        ],
+        compiler_params=pltpu.CompilerParams(collective_id=1, has_side_effects=True),
+    )(gains)
+
+
+def solve_hermitian(groups_real, groups_imag, mixed, ridge, side_real, side_imag):
+    directions = side_real.shape[0]
+    middle = directions // 2
+    row = lax.broadcasted_iota(jnp.int32, side_real.shape, 0)
+    upper = row < middle
+    swapped = pltpu.roll(mixed, middle, axis=0)
+    real = {0: groups_real[0] + ridge, middle: jnp.where(upper, mixed, swapped)}
+    imag = {0: jnp.zeros_like(ridge), middle: jnp.where(upper, -swapped, mixed)}
+    for d in range(1, middle):
+        real[d], imag[d] = groups_real[d], groups_imag[d - 1]
+        real[directions - d] = pltpu.roll(groups_real[d], d, axis=0)
+        imag[directions - d] = -pltpu.roll(groups_imag[d - 1], d, axis=0)
+    columns = []
+    for l in range(directions):
+        column_real, column_imag = real[l], imag[l]
+        for k in range(1, directions):
+            here = row == k
+            d = (l - k) % directions
+            column_real = jnp.where(here, real[d], column_real)
+            column_imag = jnp.where(here, imag[d], column_imag)
+        columns.append((column_real, column_imag))
+    columns.append((side_real, side_imag))
+    scale = jnp.zeros_like(ridge)
+    for j in range(directions):
+        pivot_real, pivot_imag = columns[j]
+        inverse = 1.0 / pivot_real[j : j + 1]
+        here = row == j
+        scale = jnp.where(here, jnp.broadcast_to(inverse, scale.shape), scale)
+        factor_real = jnp.where(here, 0.0, pivot_real * inverse)
+        factor_imag = jnp.where(here, 0.0, pivot_imag * inverse)
+        for l in range(j + 1, directions + 1):
+            value_real, value_imag = columns[l]
+            head_real, head_imag = value_real[j : j + 1], value_imag[j : j + 1]
+            columns[l] = (
+                value_real - (factor_real * head_real - factor_imag * head_imag),
+                value_imag - (factor_real * head_imag + factor_imag * head_real),
+            )
+    return columns[-1][0] * scale, columns[-1][1] * scale
+
+
+def basis_of(channel, channels):
+    x = (2.0 * channel - (channels - 1)) / max(channels - 1, 1)
+    return [
+        jnp.ones_like(x),
+        x,
+        0.5 * (3.0 * x * x - 1.0),
+        0.5 * (5.0 * x * x * x - 3.0 * x),
+    ]
+
+
+def inverse_gram(channels):
+    f = np.arange(channels, dtype=np.float64)
+    x = (2.0 * f - (channels - 1)) / max(channels - 1, 1)
+    basis = np.stack([np.ones_like(x), x, 0.5 * (3 * x * x - 1), 0.5 * (5 * x * x * x - 3 * x)])
+    return np.linalg.inv(basis @ basis.T)
+
+
+def finish_kernel(
+    chan_count,
+    sub_count,
+    half,
+    rho_ref,
+    packed_ref,
+    duals_ref,
+    consensus_ref,
+    gains_out,
+    consensus_out,
+    duals_out,
+    pad,
+    near_buf,
+    send_buf,
+    far_buf,
+    weights,
+    basis_buf,
+    near_send,
+    near_recv,
+    far_send,
+    far_recv,
+    last_send,
+    last_recv,
+):
+    chan, sub = lax.axis_index("chan"), lax.axis_index("sub")
+    owners = chan_count * sub_count
+    channels = owners * half
+    width = LANES // half
+    directions, stations = duals_ref.shape[2], duals_ref.shape[3]
+    degree = consensus_ref.shape[0]
+    me = chan * sub_count + sub
+
+    def device(flat):
+        return {"chan": lax.div(flat, sub_count), "sub": lax.rem(flat, sub_count)}
+
+    barrier = pltpu.get_barrier_semaphore()
+    for offset in range(1, owners):
+        pl.semaphore_signal(
+            barrier,
+            inc=1,
+            device_id=device(lax.rem(me + offset, owners)),
+            device_id_type=pl.DeviceIdType.MESH,
+        )
+    pl.semaphore_wait(barrier, owners - 1)
+
+    order = list(range(1, chan_count)) + [0]
+    near = {}
+    for offset in order:
+        target = lax.rem(chan + offset, chan_count)
+        for shift in range(1, sub_count):
+            other = lax.rem(sub + shift, sub_count)
+            copy = pltpu.make_async_remote_copy(
+                src_ref=packed_ref.at[target, other],
+                dst_ref=near_buf.at[shift - 1, offset],
+                send_sem=near_send.at[shift - 1, offset],
+                recv_sem=near_recv.at[shift - 1, offset],
+                device_id={"sub": other},
+                device_id_type=pl.DeviceIdType.MESH,
+            )
+            copy.start()
+            near[offset, shift] = copy
+
+    pad[...] = jnp.zeros_like(pad)
+    shape = (directions, LANES)
+    row = lax.broadcasted_iota(jnp.int32, shape, 0)
+    rho = jnp.zeros(shape, jnp.float32)
     for k in range(directions):
-        row_real, row_imag = [], []
-        for l in range(directions):
-            d = (l - k) % directions
-            if d <= half:
-                row_real.append(real[d][k])
-                row_imag.append(imag[d][k])
-            else:
-                row_real.append(real[directions - d][l])
-                row_imag.append(-imag[directions - d][l])
-        out_real.append(jnp.stack(row_real))
-        out_imag.append(jnp.stack(row_imag))
-    return jnp.stack(out_real), jnp.stack(out_imag)
-
-
-def fit_consensus(poly_basis, summed):
-    gram_matrix = jnp.dot(poly_basis, poly_basis.T, precision=lax.Precision.HIGHEST)
-    factor = jnp.linalg.cholesky(gram_matrix)
-    coeffs = jax.scipy.linalg.cho_solve((factor, True), summed.reshape(summed.shape[0], -1))
-    return coeffs.reshape(summed.shape)
+        rho = jnp.where(row == k, rho_ref[k], rho)
+    lane = lax.broadcasted_iota(jnp.int32, (owners, LANES), 1)
+    owner = lax.broadcasted_iota(jnp.int32, (owners, LANES), 0)
+    everyone = basis_of((owner * half + lax.div(lane, width)).astype(jnp.float32), channels)
+    for d in range(degree):
+        basis_buf[d] = everyone[d]
+    mine = [jnp.broadcast_to(basis_buf[d, pl.ds(me, 1), :], shape) for d in range(degree)]
+    duals = [
+        lay_pair(lambda number: duals_ref[number, part], pad, half, width) for part in range(2)
+    ]
+    anchors = []
+    for part in range(2):
+        anchor = jnp.zeros(shape, jnp.float32)
+        for d in range(degree):
+            anchor = anchor + mine[d] * lay_pair(
+                lambda number: consensus_ref[d, part], pad, half, width
+            )
+        anchors.append(anchor)
+
+    far = []
+    for offset in order:
+        target = lax.rem(chan + offset, chan_count)
+        total = packed_ref[target, sub]
+        for shift in range(1, sub_count):
+            near[offset, shift].wait_recv()
+            total = total + near_buf[shift - 1, offset]
+        if offset:
+            send_buf[offset] = total
+            copy = pltpu.make_async_remote_copy(
+                src_ref=send_buf.at[offset],
+                dst_ref=far_buf.at[offset],
+                send_sem=far_send.at[offset],
+                recv_sem=far_recv.at[offset],
+                device_id={"chan": target},
+                device_id_type=pl.DeviceIdType.MESH,
+            )
+            copy.start()
+            far.append((offset, copy))
+    for offset, copy in far:
+        copy.wait_recv()
+        total = total + far_buf[offset]
+
+    middle = directions // 2
+    group = [total[i * directions : (i + 1) * directions] for i in range(directions + 2)]
+    solved = solve_hermitian(
+        group[:middle],
+        group[middle : directions - 1],
+        group[directions - 1],
+        rho,
+        group[directions] - duals[0] + rho * anchors[0],
+        group[directions + 1] - duals[1] + rho * anchors[1],
+    )
+    for part in range(2):
+        weights[me, part] = solved[part] + duals[part] / rho
+
+    last = []
+    for offset in range(1, owners):
+        copy = pltpu.make_async_remote_copy(
+            src_ref=weights.at[me],
+            dst_ref=weights.at[me],
+            send_sem=last_send.at[offset],
+            recv_sem=last_recv.at[offset],
+            device_id=device(lax.rem(me + offset, owners)),
+            device_id_type=pl.DeviceIdType.MESH,
+        )
+        copy.start()
+        last.append(copy)
+
+    def store(ref, part, value):
+        for number in range(half):
+            turned = pltpu.roll(value, LANES - number * width, axis=1) if number else value
+            ref[number, part] = turned[:, :stations]
+
+    for part in range(2):
+        store(gains_out, part, solved[part])
+    for copy in last:
+        copy.wait_recv()
+    inverse = inverse_gram(channels)
+    for part in range(2):
+        totals = []
+        for d in range(degree):
+            value = jnp.zeros(shape, jnp.float32)
+            for number in range(owners):
+                value = value + basis_buf[d, number : number + 1, :] * weights[number, part]
+            folded = value
+            for number in range(1, half):
+                folded = folded + pltpu.roll(value, number * width, axis=1)
+            totals.append(folded)
+        fitted = jnp.zeros(shape, jnp.float32)
+        for d in range(degree):
+            value = sum(float(inverse[d, e]) * totals[e] for e in range(degree))
+            consensus_out[d, part] = value[:, :stations]
+            fitted = fitted + mine[d] * value
+        store(duals_out, part, duals[part] + rho * (solved[part] - fitted))
+    for copy in near.values():
+        copy.wait_send()
+    for _, copy in far:
+        copy.wait_send()
+    for copy in last:
+        copy.wait_send()
+
+
+def finish(rho, packed, duals, consensus, chan_count, sub_count):
+    half, _, directions, stations = duals.shape
+    _, _, rows, _ = packed.shape
+    owners = chan_count * sub_count
+    degree = consensus.shape[0]
+    vmem = pl.BlockSpec(memory_space=pltpu.VMEM)
+    dma = pltpu.SemaphoreType.DMA
+    return pl.pallas_call(
+        functools.partial(finish_kernel, chan_count, sub_count, half),
+        out_shape=(
+            jax.ShapeDtypeStruct(duals.shape, jnp.float32),
+            jax.ShapeDtypeStruct(consensus.shape, jnp.float32),
+            jax.ShapeDtypeStruct(duals.shape, jnp.float32),
+        ),
+        in_specs=[pl.BlockSpec(memory_space=pltpu.SMEM), vmem, vmem, vmem],
+        out_specs=(vmem, vmem, vmem),
+        scratch_shapes=[
+            pltpu.VMEM((2, directions, LANES), jnp.float32),
+            pltpu.VMEM((sub_count - 1, chan_count, rows, LANES), jnp.float32),
+            pltpu.VMEM((chan_count, rows, LANES), jnp.float32),
+            pltpu.VMEM((chan_count, rows, LANES), jnp.float32),
+            pltpu.VMEM((owners, 2, directions, LANES), jnp.float32),
+            pltpu.VMEM((degree, owners, LANES), jnp.float32),
+            dma((sub_count - 1, chan_count)),
+            dma((sub_count - 1, chan_count)),
+            dma((chan_count,)),
+            dma((chan_count,)),
+            dma((owners,)),
+            dma((owners,)),
+        ],
+        compiler_params=pltpu.CompilerParams(
+            collective_id=2, has_side_effects=True, vmem_limit_bytes=60 << 20
+        ),
+    )(rho, packed, duals, consensus)
 
 
 def body(
@@ -236,13 +521,11 @@
     consensus,
     rho,
 ):
-    channels_here, _, stations, directions = gains.shape
+    channels_here, _, _, directions = gains.shape
     chan_count = lax.axis_size("chan")
     sub_count = lax.axis_size("sub")
     half = channels_here // sub_count
-    turned = jnp.swapaxes(gains, 2, 3)
-    turned = jnp.pad(turned, ((0, 0), (0, 0), (0, 0), (0, LANES - stations)))
-    all_gains = lax.all_gather(turned, "chan", axis=0, tiled=True)
+    all_gains = gather_gains(jnp.swapaxes(gains, 2, 3), chan_count, sub_count)
     full_channel = tile_owner[:, 0] * channels_here + tile_channel
     packed = accumulate(
         predicted_sky_response,
@@ -253,50 +536,16 @@
         pairs,
         all_gains.reshape(-1, directions, LANES),
         half,
-        stations,
     )
-    mine = lax.psum_scatter(packed, ("chan", "sub"), scatter_dimension=0, tiled=True)[0]
-    sub_index = lax.axis_index("sub")
-    chan_index = lax.axis_index("chan")
-    poly_basis = legendre_rows(channels_here * chan_count)
-    first_channel = (chan_index * sub_count + sub_index) * half
-    my_basis = lax.dynamic_slice_in_dim(poly_basis, first_channel, half, 1)
-    anchor = jnp.einsum("df,dcsk->fcsk", my_basis, consensus, precision=lax.Precision.HIGHEST)
-    real, imag = unpack_normal(mine, directions)
-    width = LANES // half
-
-    def by_station(x):
-        x = x.reshape(x.shape[:-1] + (half, width))[..., :stations]
-        return jnp.moveaxis(x, (-2, -1), (0, 1))
-
-    real, imag = by_station(real), by_station(imag)
-    ridge = jnp.diag(rho)
-    system = jnp.concatenate(
-        [
-            jnp.concatenate([real + ridge, -imag], axis=-1),
-            jnp.concatenate([imag, real + ridge], axis=-1),
-        ],
-        axis=-2,
+    outputs = finish(
+        rho,
+        packed.reshape((chan_count, sub_count) + packed.shape[1:]),
+        jnp.swapaxes(duals, 2, 3),
+        jnp.swapaxes(consensus, 2, 3),
+        chan_count,
+        sub_count,
     )
-    side = by_station(mine[directions * directions :].reshape(2, directions, LANES))
-    duals_rows = jnp.transpose(duals, (0, 2, 1, 3))
-    anchor_rows = jnp.transpose(anchor, (0, 2, 1, 3))
-    target = side - duals_rows + rho * anchor_rows
-    factor = jnp.linalg.cholesky(system)
-    solved = jax.scipy.linalg.cho_solve(
-        (factor, True), target.reshape(half, stations, 2 * directions)[..., None]
-    )[..., 0]
-    gains_new = jnp.transpose(solved.reshape(half, stations, 2, directions), (0, 2, 1, 3))
-    partial_value = jnp.einsum(
-        "df,fcsk->dcsk", my_basis, gains_new + duals / rho, precision=lax.Precision.HIGHEST
-    )
-    summed = lax.psum(partial_value, ("chan", "sub"))
-    consensus_new = fit_consensus(poly_basis, summed)
-    duals_new = duals + rho * (
-        gains_new
-        - jnp.einsum("df,dcsk->fcsk", my_basis, consensus_new, precision=lax.Precision.HIGHEST)
-    )
-    return (gains_new, consensus_new, duals_new)
+    return tuple(jnp.swapaxes(x, 2, 3) for x in outputs)
 
 
 def solution(mesh):

time: 400 us -> 68.1 us (0.17)
  other arithmetic: 193 us -> 1.95 us
  blocking collectives: 92.2 us -> 0 us
  waiting for transfers between devices: 55.1 us -> 0 us
  Pallas kernels: 26.9 us -> 59.7 us
  between operations: 14.5 us -> 0.65 us
  local copies, waits for them, and re-layouts: 16 us -> 5.35 us
    another operation x13 -> x0, other arithmetic: 190 us -> none  [the longest x4 182 us: body(): factor = jnp.linalg.cholesky(system)]
    psum x1 -> x0, blocking collectives: 57.6 us -> none  [body(): summed = lax.psum(partial_value, ('chan', 'sub'))]
    reduce_scatter x1 -> x0, waiting for transfers between devices: 55.1 us -> none  [body(): lax.psum_scatter(packed, ('chan', 'sub'), scatter_dimension=0, tiled=True)]
    all_gather x1 -> x0, blocking collectives: 34.5 us -> none  [body(): all_gains = lax.all_gather(turned, 'chan', axis=0, tiled=True)]
    pallas_call x0 -> x2, Pallas kernels: none -> 32.7 us  [the longest x1 21.9 us: finish(): pl.pallas_call(functools.partial(finish_kernel, chan_count, sub_count, ha...]
    another operation x87 -> x0, local copies, waits for them, and re-layouts: 6.35 us -> none  [the longest x44 3.14 us: unpack_normal(): out_real.append(jnp.stack(row_real))]
    slice x5 -> x0, local copies, waits for them, and re-layouts: 4.23 us -> none  [the longest x2 1.73 us: unpack_normal(): row_real.append(real[d][k])]
  transfers between devices with their start and end apart: 1 -> 0, of which waited for: 1 -> 0; matrix products, arithmetic and copies ran while one was open for 1% -> 0% of each run, Pallas kernels for 0% -> 0%
where the time goes in v2:
time: 68.1 us; the launch traced here: 67.6 us
  Pallas kernels  59.7 us (88%)
  local copies, waits for them, and re-layouts  5.35 us (8%)
  other arithmetic  1.95 us (3%)
    pallas_call x1, Pallas kernels, accumulate(): pl.pallas_call(kernel, grid_spec=pltpu.PrefetchScalarGridSpec(num_scalar_...  27 us
    pallas_call x1, Pallas kernels, finish(): pl.pallas_call(functools.partial(finish_kernel, chan_count, sub_count, ha...  21.9 us
    pallas_call x1, Pallas kernels, gather_gains(): pl.pallas_call(functools.partial(gather_kernel, chan_count, sub_count, ha...  10.8 us
    unnamed x3, local copies, waits for them, and re-layouts  4.02 us

profile of v2, /device:TPU:0, one launch (start us, length us, event | category | flops | bytes accessed | tf_op | source)
XLA Modules:
  0.0 67.6 jit_solution(16763477213892426096)
XLA Ops:
  0.6 0.7 %broadcast_multiply_fusion = s32[512,1]{0,1:T(1,128)S(1)} fusion(s32[512,1]{0,1:T(1,128)} %param.14), kind=kLoop, calls=%fused_computation | loop fusion | flops 512 | bytes 4096 | tf_op jit(solution)/shard_map/mul | solution.py:529
  1.3 1.3 %add.3.channel_ref = s32[512]{0:T(512)} add(s32[512]{0:T(512)S(1)} %bitcast.21, s32[512]{0:T(512)} %param.15) | non-fusion elementwise | flops 512 | bytes 6144 | tf_op jit(solution)/shard_map/add | solution.py:529
  2.6 1.3 %reshape.25.pairs_ref = s32[30,128]{1,0:T(8,128)} reshape(s32[15,2,128]{2,1,0:T(2,128)} %param.17) | data formatting | bytes 30720 | tf_op jit(solution)/shard_map/reshape | solution.py:179
  3.9 10.8 %shard_map.130 = f32[8,2,2,8,128]{4,3,2,1,0:T(8,128)} custom-call(f32[4,2,8,62]{3,2,1,0:T(8,128)} %bitcast.15), custom_call_target="tpu_custom_call" | custom-call | tf_op jit(solution)/shard_map/pallas_call | solution.py:233
  14.7 27.0 %shard_map.131 = f32[16,80,128]{2,1,0:T(8,128)} custom-call(s32[512]{0:T(512)} %add.3.channel_ref, s32[512]{0:T(512)} %base_ref.1, bf16[8192,128]{1,0:T(8,128)(2,1)} %bitcast.12, bf16[1024,128]{1,0:T(8,128)(2,1)} %bitcast.14, s32[512,128]{1,0:T(8,128)} %keep_ref.1, s32[30,128]{1,0:T(8,128)} %reshape.25.pairs_ref, f32[32,8,128]{2,1,0:T(8,128)} %bitcast.13), custom_call_target="tpu_custom_call" | custom-call | tf_op jit(solution)/shard_map/pallas_call | solution.py:146
  41.7 21.9 %shard_map.132 = (f32[2,2,8,62]{3,2,1,0:T(8,128)}, f32[4,2,8,62]{3,2,1,0:T(8,128)}, f32[2,2,8,62]{3,2,1,0:T(8,128)}) custom-call(f32[8]{0:T(128)} %rho_ref.1, f32[8,2,80,128]{3,2,1,0:T(8,128)} %bitcast.11, f32[2,2,8,62]{3,2,1,0:T(8,128)} %bitcast.18, f32[4,2,8,62]{3,2,1,0:T(8,128)} %bitcast.16), custom_call_target="tpu_custom_call" | custom-call | tf_op jit(solution)/shard_map/pallas_call | solution.py:482
  63.6 1.3 %copy.17 = f32[2,2,62,8]{2,3,1,0:T(8,128)} copy(f32[2,2,62,8]{2,3,1,0:T(8,128)} %bitcast.20) | data formatting | bytes 15872
  64.9 1.4 %copy.18 = f32[4,2,62,8]{2,3,1,0:T(8,128)} copy(f32[4,2,62,8]{2,3,1,0:T(8,128)} %bitcast.17) | data formatting | bytes 31744
  66.3 1.3 %copy.19 = f32[2,2,62,8]{2,3,1,0:T(8,128)} copy(f32[2,2,62,8]{2,3,1,0:T(8,128)} %bitcast.19) | data formatting | bytes 15872

commit v3 on v2

--- a/solution.py
+++ b/solution.py
@@ -1,4 +1,5 @@
 import functools
+import math
 
 import jax
 import jax.numpy as jnp
@@ -28,6 +29,8 @@
     block,
     unroll,
     half,
+    sub_count,
+    owner_ref,
     channel_ref,
     base_ref,
     coupling_ref,
@@ -43,7 +46,7 @@
     keep_f,
 ):
     step = pl.program_id(0)
-    bases = pairs_ref.shape[0] // 2
+    bases = pairs_ref.shape[0]
     tile_rows = keep_ref.shape[1]
     width = LANES // half
     directions = gains_ref.shape[1]
@@ -52,15 +55,18 @@
     def _():
         out_ref[...] = jnp.zeros_like(out_ref)
         turned[...] = jnp.zeros_like(turned)
-        turned[: 2 * bases, :] = pairs_ref[...].astype(jnp.float32)
+        for base in range(bases):
+            turned[2 * base : 2 * base + 2, :] = pairs_ref[base].astype(jnp.float32)
         columns = jnp.transpose(turned[...])
         lane = lax.broadcasted_iota(jnp.int32, (tile_rows, LANES), 1).astype(jnp.float32)
         for base in range(bases):
             for end in range(2):
-                station = columns[:, 2 * base + end : 2 * base + end + 1]
+                station = jnp.broadcast_to(
+                    columns[:, 2 * base + end : 2 * base + end + 1], lane.shape
+                )
                 for part in range(half):
                     table[base * half + part, end * tile_rows : (end + 1) * tile_rows, :] = (
-                        jnp.where(station + float(part * width) == lane, 1.0, 0.0).astype(jnp.bfloat16)
+                        jnp.where(station == lane - float(part * width), 1.0, 0.0).astype(jnp.bfloat16)
                     )
 
     coupling_f[...] = coupling_ref[...].astype(jnp.float32)
@@ -75,16 +81,16 @@
         tile = step * block + local
         channel = channel_ref[tile]
         base = base_ref[tile]
+        owner = owner_ref[tile] * sub_count + lax.div(channel, half)
+        place = lax.rem(channel, half)
         kept = spread(keep_f[pl.ds(local, 1), :])
         first = local * 2 * directions
         real = coupling_f[pl.ds(first, directions, stride=2), :] * kept
         imag = coupling_f[pl.ds(first + 1, directions, stride=2), :] * kept
         seen_real = spread(observed_f[pl.ds(2 * local, 1), :])
         seen_imag = spread(observed_f[pl.ds(2 * local + 1, 1), :])
-        near = spread(pairs_ref[pl.ds(2 * base, 1), :])
-        far = spread(pairs_ref[pl.ds(2 * base + 1, 1), :])
-        place = lax.rem(channel, half)
-        owner = lax.div(channel, half)
+        near = spread(pairs_ref[base, pl.ds(0, 1), :])
+        far = spread(pairs_ref[base, pl.ds(1, 1), :])
         near, far = near + place * width, far + place * width
         gain_real = gains_ref[2 * owner]
         gain_imag = gains_ref[2 * owner + 1]
@@ -135,24 +141,24 @@
     lax.fori_loop(0, block // unroll, one_group, 0)
 
 
-def accumulate(coupling, observed, keep, channel, base, pairs, gain_table, half):
+def accumulate(coupling, observed, keep, owner, channel, base, pairs, gain_table, half, sub_count):
     tiles, directions, _, tile_rows = coupling.shape
     owners = gain_table.shape[0] // 2
     bases = pairs.shape[0]
     block = min(64, tiles)
-    unroll = 8
-    kernel = functools.partial(accumulate_kernel, block, unroll, half)
+    unroll = math.gcd(block, 32)
+    kernel = functools.partial(accumulate_kernel, block, unroll, half, sub_count)
     out_rows = directions * directions + 2 * directions
     return pl.pallas_call(
         kernel,
         grid_spec=pltpu.PrefetchScalarGridSpec(
-            num_scalar_prefetch=2,
+            num_scalar_prefetch=3,
             grid=(tiles // block,),
             in_specs=[
                 pl.BlockSpec((block * 2 * directions, tile_rows), lambda i, *_: (i, 0)),
                 pl.BlockSpec((block * 2, tile_rows), lambda i, *_: (i, 0)),
                 pl.BlockSpec((block, tile_rows), lambda i, *_: (i, 0)),
-                pl.BlockSpec((2 * bases, tile_rows), lambda i, *_: (0, 0)),
+                pl.BlockSpec(pairs.shape, lambda i, *_: (0, 0, 0)),
                 pl.BlockSpec(gain_table.shape, lambda i, *_: (0, 0, 0)),
             ],
             out_specs=pl.BlockSpec(
@@ -171,12 +177,13 @@
             dimension_semantics=("arbitrary",), vmem_limit_bytes=60 << 20
         ),
     )(
+        owner,
         channel,
         base,
         coupling.reshape(tiles * 2 * directions, tile_rows),
         observed.reshape(tiles * 2, tile_rows),
         keep,
-        pairs.reshape(2 * bases, tile_rows),
+        pairs,
         gain_table,
     )
 
@@ -303,6 +310,22 @@
     return np.linalg.inv(basis @ basis.T)
 
 
+def encode(sums, directions):
+    normal_rows = directions * directions
+    side = sums[normal_rows:]
+    high = side.astype(jnp.bfloat16)
+    low = (side - high.astype(jnp.float32)).astype(jnp.bfloat16)
+    return jnp.concatenate([sums[:normal_rows].astype(jnp.bfloat16), high, low], axis=0)
+
+
+def decode(coded, directions):
+    wide = coded.astype(jnp.float32)
+    normal_rows = directions * directions
+    side_rows = 2 * directions
+    high, low = wide[normal_rows : normal_rows + side_rows], wide[normal_rows + side_rows :]
+    return jnp.concatenate([wide[:normal_rows], high + low], axis=0)
+
+
 def finish_kernel(
     chan_count,
     sub_count,
@@ -315,6 +338,7 @@
     consensus_out,
     duals_out,
     pad,
+    near_src,
     near_buf,
     send_buf,
     far_buf,
@@ -346,16 +370,21 @@
             device_id=device(lax.rem(me + offset, owners)),
             device_id_type=pl.DeviceIdType.MESH,
         )
-    pl.semaphore_wait(barrier, owners - 1)
-
     order = list(range(1, chan_count)) + [0]
-    near = {}
     for offset in order:
         target = lax.rem(chan + offset, chan_count)
         for shift in range(1, sub_count):
+            near_src[shift - 1, offset] = encode(
+                packed_ref[target, lax.rem(sub + shift, sub_count)], directions
+            )
+    pl.semaphore_wait(barrier, owners - 1)
+
+    near = {}
+    for offset in order:
+        for shift in range(1, sub_count):
             other = lax.rem(sub + shift, sub_count)
             copy = pltpu.make_async_remote_copy(
-                src_ref=packed_ref.at[target, other],
+                src_ref=near_src.at[shift - 1, offset],
                 dst_ref=near_buf.at[shift - 1, offset],
                 send_sem=near_send.at[shift - 1, offset],
                 recv_sem=near_recv.at[shift - 1, offset],
@@ -395,9 +424,9 @@
         total = packed_ref[target, sub]
         for shift in range(1, sub_count):
             near[offset, shift].wait_recv()
-            total = total + near_buf[shift - 1, offset]
+            total = total + decode(near_buf[shift - 1, offset], directions)
         if offset:
-            send_buf[offset] = total
+            send_buf[offset] = encode(total, directions)
             copy = pltpu.make_async_remote_copy(
                 src_ref=send_buf.at[offset],
                 dst_ref=far_buf.at[offset],
@@ -410,7 +439,7 @@
             far.append((offset, copy))
     for offset, copy in far:
         copy.wait_recv()
-        total = total + far_buf[offset]
+        total = total + decode(far_buf[offset], directions)
 
     middle = directions // 2
     group = [total[i * directions : (i + 1) * directions] for i in range(directions + 2)]
@@ -477,6 +506,7 @@
     _, _, rows, _ = packed.shape
     owners = chan_count * sub_count
     degree = consensus.shape[0]
+    coded = rows + 2 * directions
     vmem = pl.BlockSpec(memory_space=pltpu.VMEM)
     dma = pltpu.SemaphoreType.DMA
     return pl.pallas_call(
@@ -490,9 +520,10 @@
         out_specs=(vmem, vmem, vmem),
         scratch_shapes=[
             pltpu.VMEM((2, directions, LANES), jnp.float32),
-            pltpu.VMEM((sub_count - 1, chan_count, rows, LANES), jnp.float32),
-            pltpu.VMEM((chan_count, rows, LANES), jnp.float32),
-            pltpu.VMEM((chan_count, rows, LANES), jnp.float32),
+            pltpu.VMEM((sub_count - 1, chan_count, coded, LANES), jnp.bfloat16),
+            pltpu.VMEM((sub_count - 1, chan_count, coded, LANES), jnp.bfloat16),
+            pltpu.VMEM((chan_count, coded, LANES), jnp.bfloat16),
+            pltpu.VMEM((chan_count, coded, LANES), jnp.bfloat16),
             pltpu.VMEM((owners, 2, directions, LANES), jnp.float32),
             pltpu.VMEM((degree, owners, LANES), jnp.float32),
             dma((sub_count - 1, chan_count)),
@@ -526,16 +557,17 @@
     sub_count = lax.axis_size("sub")
     half = channels_here // sub_count
     all_gains = gather_gains(jnp.swapaxes(gains, 2, 3), chan_count, sub_count)
-    full_channel = tile_owner[:, 0] * channels_here + tile_channel
     packed = accumulate(
         predicted_sky_response,
         measured_correlation,
         keep_indicator,
-        full_channel,
+        tile_owner[:, 0],
+        tile_channel,
         tile_base,
         pairs,
         all_gains.reshape(-1, directions, LANES),
         half,
+        sub_count,
     )
     outputs = finish(
         rho,

time: 68.1 us -> 53.3 us (0.78)
  Pallas kernels: 59.7 us -> 48.2 us
  other arithmetic: 1.95 us -> 0 us
  local copies, waits for them, and re-layouts: 5.35 us -> 4.02 us
    pallas_call x1, Pallas kernels: 27 us -> 18.4 us  [accumulate(): pl.pallas_call(kernel, grid_spec=pltpu.PrefetchScalarGridSpec(num_scalar_...]
    pallas_call x1, Pallas kernels: 21.9 us -> 18.9 us  [finish(): pl.pallas_call(functools.partial(finish_kernel, chan_count, sub_count, ha...]
    reshape x1 -> x0, local copies, waits for them, and re-layouts: 1.33 us -> none  [accumulate(): pairs.reshape(2 * bases, tile_rows)]
    add x1 -> x0, other arithmetic: 1.26 us -> none  [body(): full_channel = tile_owner[:, 0] * channels_here + tile_channel]
    mul x1 -> x0, other arithmetic: 0.69 us -> none  [body(): full_channel = tile_owner[:, 0] * channels_here + tile_channel]
where the time goes in v3:
time: 53.3 us; the launch traced here: 52.8 us
  Pallas kernels  48.2 us (90%)
  local copies, waits for them, and re-layouts  4.02 us (8%)
  between operations  0.65 us (1%)
    pallas_call x1, Pallas kernels, finish(): pl.pallas_call(functools.partial(finish_kernel, chan_count, sub_count, ha...  18.9 us
    pallas_call x1, Pallas kernels, accumulate(): pl.pallas_call(kernel, grid_spec=pltpu.PrefetchScalarGridSpec(num_scalar_...  18.4 us
    pallas_call x1, Pallas kernels, gather_gains(): pl.pallas_call(functools.partial(gather_kernel, chan_count, sub_count, ha...  10.8 us
    unnamed x3, local copies, waits for them, and re-layouts  4.02 us

profile of v3, /device:TPU:0, one launch (start us, length us, event | category | flops | bytes accessed | tf_op | source)
XLA Modules:
  0.0 52.8 jit_solution(12101244111537770314)
XLA Ops:
  0.6 10.8 %shard_map.130 = f32[8,2,2,8,128]{4,3,2,1,0:T(8,128)} custom-call(f32[4,2,8,62]{3,2,1,0:T(8,128)} %bitcast.15), custom_call_target="tpu_custom_call" | custom-call | tf_op jit(solution)/shard_map/pallas_call | solution.py:240
  11.5 18.4 %shard_map.131 = f32[16,80,128]{2,1,0:T(8,128)} custom-call(s32[512]{0:T(512)} %bitcast.21, s32[512]{0:T(512)} %channel_ref.1, s32[512]{0:T(512)} %base_ref.1, bf16[8192,128]{1,0:T(8,128)(2,1)} %bitcast.12, bf16[1024,128]{1,0:T(8,128)(2,1)} %bitcast.14, s32[512,128]{1,0:T(8,128)} %keep_ref.1, s32[15,2,128]{2,1,0:T(2,128)} %pairs_ref.1, f32[32,8,128]{2,1,0:T(8,128)} %bitcast.13), custom_call_target="tpu_custom_call" | custom-call | tf_op jit(solution)/shard_map/pallas_call | solution.py:152
  29.9 18.9 %shard_map.132 = (f32[2,2,8,62]{3,2,1,0:T(8,128)}, f32[4,2,8,62]{3,2,1,0:T(8,128)}, f32[2,2,8,62]{3,2,1,0:T(8,128)}) custom-call(f32[8]{0:T(128)} %rho_ref.1, f32[8,2,80,128]{3,2,1,0:T(8,128)} %bitcast.11, f32[2,2,8,62]{3,2,1,0:T(8,128)} %bitcast.18, f32[4,2,8,62]{3,2,1,0:T(8,128)} %bitcast.16), custom_call_target="tpu_custom_call" | custom-call | tf_op jit(solution)/shard_map/pallas_call | solution.py:512
  48.8 1.3 %copy.17 = f32[2,2,62,8]{2,3,1,0:T(8,128)} copy(f32[2,2,62,8]{2,3,1,0:T(8,128)} %bitcast.20) | data formatting | bytes 15872
  50.1 1.4 %copy.18 = f32[4,2,62,8]{2,3,1,0:T(8,128)} copy(f32[4,2,62,8]{2,3,1,0:T(8,128)} %bitcast.17) | data formatting | bytes 31744
  51.5 1.3 %copy.19 = f32[2,2,62,8]{2,3,1,0:T(8,128)} copy(f32[2,2,62,8]{2,3,1,0:T(8,128)} %bitcast.19) | data formatting | bytes 15872

commit v4 on v3

--- a/solution.py
+++ b/solution.py
@@ -146,7 +146,7 @@
     owners = gain_table.shape[0] // 2
     bases = pairs.shape[0]
     block = min(64, tiles)
-    unroll = math.gcd(block, 32)
+    unroll = math.gcd(block, 64)
     kernel = functools.partial(accumulate_kernel, block, unroll, half, sub_count)
     out_rows = directions * directions + 2 * directions
     return pl.pallas_call(

time: 53.3 us -> 52.8 us (level)
  no operation moved by 1% of the time
where the time goes in v4:
time: 52.8 us; the launch traced here: 52.3 us
  Pallas kernels  47.7 us (90%)
  local copies, waits for them, and re-layouts  4.02 us (8%)
  between operations  0.65 us (1%)
    pallas_call x1, Pallas kernels, finish(): pl.pallas_call(functools.partial(finish_kernel, chan_count, sub_count, ha...  18.9 us
    pallas_call x1, Pallas kernels, accumulate(): pl.pallas_call(kernel, grid_spec=pltpu.PrefetchScalarGridSpec(num_scalar_...  17.9 us
    pallas_call x1, Pallas kernels, gather_gains(): pl.pallas_call(functools.partial(gather_kernel, chan_count, sub_count, ha...  10.8 us
    unnamed x3, local copies, waits for them, and re-layouts  4.02 us

profile of v4, /device:TPU:0, one launch (start us, length us, event | category | flops | bytes accessed | tf_op | source)
XLA Modules:
  0.0 52.3 jit_solution(6191325881042279324)
XLA Ops:
  0.6 10.8 %shard_map.130 = f32[8,2,2,8,128]{4,3,2,1,0:T(8,128)} custom-call(f32[4,2,8,62]{3,2,1,0:T(8,128)} %bitcast.15), custom_call_target="tpu_custom_call" | custom-call | tf_op jit(solution)/shard_map/pallas_call | solution.py:240
  11.5 17.9 %shard_map.131 = f32[16,80,128]{2,1,0:T(8,128)} custom-call(s32[512]{0:T(512)} %bitcast.21, s32[512]{0:T(512)} %channel_ref.1, s32[512]{0:T(512)} %base_ref.1, bf16[8192,128]{1,0:T(8,128)(2,1)} %bitcast.12, bf16[1024,128]{1,0:T(8,128)(2,1)} %bitcast.14, s32[512,128]{1,0:T(8,128)} %keep_ref.1, s32[15,2,128]{2,1,0:T(2,128)} %pairs_ref.1, f32[32,8,128]{2,1,0:T(8,128)} %bitcast.13), custom_call_target="tpu_custom_call" | custom-call | tf_op jit(solution)/shard_map/pallas_call | solution.py:152
  29.4 18.9 %shard_map.132 = (f32[2,2,8,62]{3,2,1,0:T(8,128)}, f32[4,2,8,62]{3,2,1,0:T(8,128)}, f32[2,2,8,62]{3,2,1,0:T(8,128)}) custom-call(f32[8]{0:T(128)} %rho_ref.1, f32[8,2,80,128]{3,2,1,0:T(8,128)} %bitcast.11, f32[2,2,8,62]{3,2,1,0:T(8,128)} %bitcast.18, f32[4,2,8,62]{3,2,1,0:T(8,128)} %bitcast.16), custom_call_target="tpu_custom_call" | custom-call | tf_op jit(solution)/shard_map/pallas_call | solution.py:512
  48.3 1.3 %copy.17 = f32[2,2,62,8]{2,3,1,0:T(8,128)} copy(f32[2,2,62,8]{2,3,1,0:T(8,128)} %bitcast.20) | data formatting | bytes 15872
  49.6 1.4 %copy.18 = f32[4,2,62,8]{2,3,1,0:T(8,128)} copy(f32[4,2,62,8]{2,3,1,0:T(8,128)} %bitcast.17) | data formatting | bytes 31744
  51.0 1.3 %copy.19 = f32[2,2,62,8]{2,3,1,0:T(8,128)} copy(f32[2,2,62,8]{2,3,1,0:T(8,128)} %bitcast.19) | data formatting | bytes 15872
